TPU v7x, 32 devices: a whole 2x2x4 slice. The times are simulated.
32 devices in a mesh: patch: 8 (over z, y), hidden: 4 (over x, core).
Axes of the slice: x: 2, y: 2, z: 4, core: 2. Of those that a mesh axis runs over, the one named last changes fastest.
Arguments:
- nodes: bfloat16 [16384, 512], P('patch', 'hidden'), may hold values from -6 to 6
- edges: bfloat16 [65536, 512], P(('patch', 'hidden')), may hold values from -6 to 6
- senders: int32 [65536], P(('patch', 'hidden')), may hold values from 0 to 4159
- receivers: int32 [65536], P(('patch', 'hidden')), may hold values from 0 to 2047
- halo_rows: int32 [8, 2, 1024], P('patch'), may hold values from 0 to 2047
- coarse_rows: int32 [8, 8, 8], P('patch'), may hold values from 0 to 63
- edge_count: int32 [32], P(('patch', 'hidden')), may hold values from 1024 to 2048, as said below
- w_edge_in: bfloat16 [1536, 512], replicated, may hold values from -0.15625 to 0.15625
- b_edge_in: float32 [512], replicated, may hold values from -3 to 3
- w_edge_out: bfloat16 [512, 512], replicated, may hold values from -0.25 to 0.25
- b_edge_out: float32 [512], replicated, may hold values from -2 to 2
- edge_gain: float32 [512], replicated, may hold values from 0.5 to 1.5
- edge_shift: float32 [512], replicated, may hold values from -1 to 1
- w_node_in: bfloat16 [1024, 512], replicated, may hold values from -0.1875 to 0.1875
- b_node_in: float32 [512], replicated, may hold values from -3 to 3
- w_node_out: bfloat16 [512, 512], replicated, may hold values from -0.25 to 0.25
- b_node_out: float32 [512], replicated, may hold values from -2 to 2
- node_gain: float32 [512], replicated, may hold values from 0.5 to 1.5
- node_shift: float32 [512], replicated, may hold values from -1 to 1
Outputs:
- nodes_out: bfloat16 [16384, 512], P('patch', 'hidden')
- edges_out: bfloat16 [65536, 512], P(('patch', 'hidden'))
Inputs may be any that keep to these rules, and one draw needn't show every extreme that they name: `edge_count`: some block holds 2048 live edges.
All inputs are finite; a program needn't handle non-finite values.
Results may differ from a plain program's by a relative error of at most 0.007.
Values may be sent and summed in bfloat16 or wider, within the bound.
A program may use at most 128 MiB of HBM per device.

v0:
```python
import jax
import jax.numpy as jnp
from jax import lax
from jax.sharding import PartitionSpec as P

layer_epsilon = 1e-05


def extended(block, sides, width):
    for axis, dim in sides:
        count = lax.axis_size(axis)
        forward = [(i, i + 1) for i in range(count - 1)]
        forward.append((count - 1, 0))
        backward = [(target, source) for source, target in forward]
        low = lax.ppermute(
            lax.slice_in_dim(block, block.shape[dim] - width, None, axis=dim), axis, forward
        )
        high = lax.ppermute(lax.slice_in_dim(block, 0, width, axis=dim), axis, backward)
        block = jnp.concatenate([low, block, high], axis=dim)
    return block


def normalize(output, norm_gain, norm_shift):
    row_mean = jnp.mean(output, axis=1, keepdims=True)
    row_var = jnp.mean(jnp.square(output - row_mean), axis=1, keepdims=True)
    return (output - row_mean) * lax.rsqrt(row_var + layer_epsilon) * norm_gain + norm_shift


def local(
    nodes,
    edges,
    senders,
    receivers,
    halo_rows,
    coarse_rows,
    edge_count,
    w_edge_in,
    b_edge_in,
    w_edge_out,
    b_edge_out,
    edge_gain,
    edge_shift,
    w_node_in,
    b_node_in,
    w_node_out,
    b_node_out,
    node_gain,
    node_shift,
):
    own_block = lax.all_gather(nodes, "hidden", axis=1, tiled=True)
    node_rows = own_block.shape[0]
    columns = own_block.shape[1]
    border_rows = halo_rows.shape[2]
    outgoing = jnp.concatenate([own_block[halo_rows[0, 0]], own_block[halo_rows[0, 1]]], axis=0)
    bordered = extended(outgoing, (("patch", 0),), border_rows)
    requested = lax.all_to_all(coarse_rows[0], "patch", split_axis=0, concat_axis=0, tiled=True)
    replies = lax.all_to_all(own_block[requested], "patch", split_axis=0, concat_axis=0, tiled=True)
    distant = replies.reshape(-1, columns)
    sender_table = jnp.concatenate(
        [own_block, bordered[:border_rows], bordered[3 * border_rows :], distant], axis=0
    )
    live_count = edge_count[0]
    edge_rows = edges.shape[0]
    block_rows = 512
    weight_self = w_edge_in[:columns]
    weight_send = w_edge_in[columns : 2 * columns]
    weight_target = w_edge_in[2 * columns :]
    node_index = jnp.arange(node_rows, dtype=jnp.int32)

    def edge_block(summed, position):
        offset = position * block_rows
        latent = lax.dynamic_slice_in_dim(edges, offset, block_rows, 0)
        sender_code = lax.dynamic_slice_in_dim(senders, offset, block_rows, 0)
        target = lax.dynamic_slice_in_dim(receivers, offset, block_rows, 0)
        onehot = (target[:, None] == node_index[None, :]).astype(jnp.bfloat16)
        receiver_rows = jnp.dot(onehot, own_block, preferred_element_type=jnp.float32).astype(
            jnp.bfloat16
        )
        pre_active = jnp.dot(latent, weight_self, preferred_element_type=jnp.float32)
        pre_active = pre_active + jnp.dot(
            sender_table[sender_code], weight_send, preferred_element_type=jnp.float32
        )
        pre_active = (
            pre_active
            + jnp.dot(receiver_rows, weight_target, preferred_element_type=jnp.float32)
            + b_edge_in
        )
        active = jax.nn.silu(pre_active).astype(jnp.bfloat16)
        output = jnp.dot(active, w_edge_out, preferred_element_type=jnp.float32) + b_edge_out
        update = normalize(output, edge_gain, edge_shift)
        live_mask = offset + jnp.arange(block_rows, dtype=jnp.int32) < live_count
        message = jnp.where(live_mask[:, None], update, jnp.zeros_like(update))
        new_latent = (latent.astype(jnp.float32) + message).astype(jnp.bfloat16)
        summed = summed + lax.dot_general(
            onehot,
            message.astype(jnp.bfloat16),
            (((0,), (0,)), ((), ())),
            preferred_element_type=jnp.float32,
        )
        return (summed, new_latent)

    summed, pieces = lax.scan(
        edge_block,
        jnp.zeros((node_rows, columns), jnp.float32),
        jnp.arange(edge_rows // block_rows, dtype=jnp.int32),
    )
    edges_out = pieces.reshape(edge_rows, columns)
    aggregated = lax.psum_scatter(
        summed.astype(jnp.bfloat16), "hidden", scatter_dimension=0, tiled=True
    ).astype(jnp.float32)
    share_rows = aggregated.shape[0]
    own_rows = lax.dynamic_slice_in_dim(
        own_block, lax.axis_index("hidden") * share_rows, share_rows, 0
    )
    pre_active = jnp.dot(own_rows, w_node_in[:columns], preferred_element_type=jnp.float32)
    pre_active = (
        pre_active
        + jnp.dot(
            aggregated.astype(jnp.bfloat16), w_node_in[columns:], preferred_element_type=jnp.float32
        )
        + b_node_in
    )
    active = jax.nn.silu(pre_active).astype(jnp.bfloat16)
    output = jnp.dot(active, w_node_out, preferred_element_type=jnp.float32) + b_node_out
    update = normalize(output, node_gain, node_shift)
    new_rows = (own_rows.astype(jnp.float32) + update).astype(jnp.bfloat16)
    nodes_out = lax.all_to_all(new_rows, "hidden", split_axis=1, concat_axis=0, tiled=True)
    return (nodes_out, edges_out)


def solution(mesh):
    return jax.shard_map(
        local,
        mesh=mesh,
        in_specs=(
            P("patch", "hidden"),
            P(("patch", "hidden"), None),
            P(("patch", "hidden")),
            P(("patch", "hidden")),
            P("patch", None, None),
            P("patch", None, None),
            P(("patch", "hidden")),
            P(),
            P(),
            P(),
            P(),
            P(),
            P(),
            P(),
            P(),
            P(),
            P(),
            P(),
            P(),
        ),
        out_specs=(P("patch", "hidden"), P(("patch", "hidden"), None)),
        check_vma=False,
    )
```

profile of v0, /device:TPU:0, one launch (start us, length us, event | category | flops | bytes accessed | tf_op | source)
XLA Modules:
  0.0 276.9 jit_solution(9860688080146341400)
XLA Ops:
  7.2 2.1 copy.45
  9.3 0.8 compare_select_fusion.2
  10.2 25.3 %all-gather.2.cloned.1.call-done = bf16[2048,512]{0,1:T(8,128)(2,1)} async-done(((bf16[2048,128]{0,1:T(8,128)(2,1)}), bf16[2048,512]{0,1:T(8,128)(2,1)}) %all-gather.2.cloned.1.call-update) | async-done | bytes 2097168 | tf_op jit(solution)/shard_map/all_gather | solution.py:50
  35.4 3.9 %copy.46 = bf16[2048,512]{1,0:T(8,128)(2,1)} copy(bf16[2048,512]{0,1:T(8,128)(2,1)} %all-gather.2.cloned.1.call-done) | data formatting | bytes 4194304 | tf_op jit(solution)/shard_map/all_gather | solution.py:50
  39.3 5.8 %gather_fusion.1 = bf16[1024,512]{1,0:T(8,128)(2,1)S(1)} fusion(bf16[2048,512]{1,0:T(8,128)(2,1)} %copy.46, s32[1024]{0:T(1024)S(1)} %broadcast_clamp_fusion.1), kind=kCustom, calls=%fused_computation.1 | custom fusion | bytes 2101248 | tf_op jit(solution)/shard_map/gather | solution.py:54
  45.2 1.3 copy.47
  46.5 1.5 collective-permute-start
  48.0 5.8 %gather_fusion.2 = bf16[1024,512]{1,0:T(8,128)(2,1)S(1)} fusion(bf16[2048,512]{1,0:T(8,128)(2,1)} %copy.46, s32[1024]{0:T(1024)S(1)} %broadcast_clamp_fusion), kind=kCustom, calls=%fused_computation.2 | custom fusion | bytes 2101248 | tf_op jit(solution)/shard_map/gather | solution.py:54
  53.9 1.4 copy.49
  55.2 3.3 %collective-permute-start.1 = (bf16[1024,512]{0,1:T(8,128)(2,1)}, bf16[1024,512]{0,1:T(8,128)(2,1)}, u32[]{:S(2)}, u32[]{:S(2)}) collective-permute-start(bf16[1024,512]{0,1:T(8,128)(2,1)} %copy.49), channel_id=1, source_target_pairs={{4,0},{8,4},{12,8},{16,12},{20,16},{24,20},{28,24},{0,28},{5,1},{9... | collective-permute-start | bytes 3145736 | tf_op jit(solution)/shard_map/ppermute | solution.py:18
  58.5 38.8 %all_to_all.36 = s32[8,1,8]{2,1,0:T(1,128)S(1)} all-to-all(s32[8,1,8]{2,1,0:T(1,128)S(1)} %bitcast.59), channel_id=1, replica_groups=mesh['patch'=8,'hidden'=4] {'patch'}, dimensions={0} | all-to-all | bytes 512 | tf_op jit(solution)/shard_map/all_to_all | solution.py:56
  97.4 3.2 %gather_fusion.3 = bf16[64,512]{1,0:T(8,128)(2,1)} fusion(bf16[2048,512]{1,0:T(8,128)(2,1)} %copy.46, s32[1024]{0:T(1024)S(1)} %pad_clamp_fusion.1), kind=kCustom, calls=%fused_computation.3 | custom fusion | bytes 131328 | tf_op jit(solution)/shard_map/gather | solution.py:57
  100.6 3.3 %all-to-all-start.1 = ((bf16[8,8,512]{2,1,0:T(8,128)(2,1)}), bf16[8,8,512]{2,1,0:T(8,128)(2,1)S(1)}, u32[]{:S(2)}, u32[]{:S(2)}) async-start(bf16[8,8,512]{2,1,0:T(8,128)(2,1)} %bitcast.8), calls=%async_computation.1 | async-start | bytes 131072 | tf_op jit(solution)/shard_map/all_to_all | solution.py:57
  104.2 0.9 fusion.33
  105.1 5.7 %all-to-all-done.1 = bf16[8,8,512]{2,1,0:T(8,128)(2,1)S(1)} async-done(((bf16[8,8,512]{2,1,0:T(8,128)(2,1)}), bf16[8,8,512]{2,1,0:T(8,128)(2,1)S(1)}, u32[]{:S(2)}, u32[]{:S(2)}) %all-to-all-start.1) | async-done | bytes 65568 | tf_op jit(solution)/shard_map/all_to_all | solution.py:57
  111.0 3.7 %pad_maximum_fusion = bf16[4160,512]{0,1:T(8,128)(2,1)} fusion(bf16[64,512]{0,1:T(8,128)(2,1)S(1)} %copy.52, bf16[1024,512]{0,1:T(8,128)(2,1)} %collective-permute-done.1, bf16[1024,512]{0,1:T(8,128)(2,1)} %collective-permute-done, bf16[2048,512]{0,1:T(8,128)(2,1)} %all-gather.2.cloned.1.call-done), kind=kLoop, calls=%fused_computation.39 | loop fusion | flops 17039360 | bytes 8519680 | tf_op jit(solution)/shard_map/concatenate | solution.py:59
  114.7 6.6 %copy.54 = bf16[4160,512]{1,0:T(8,128)(2,1)} copy(bf16[4160,512]{0,1:T(8,128)(2,1)} %pad_maximum_fusion) | data formatting | bytes 8519680
  121.3 98.3 %while.13 = (s32[]{:T(128)}, f32[2048,512]{1,0:T(8,128)}, bf16[4,512,512]{2,1,0:T(8,128)(2,1)}, s32[4]{0:T(128)S(1)}, s32[2048]{0:T(1024)}, /*index=5*/s32[]{:T(...) while((s32[]{:T(128)}, f32[2048,512]{1,0:T(8,128)}, ...), condition=%wide.region_3.4_spmd.clone, body=%wide.region_0.3_spmd.clone.sunk | while | flops 3233812480 | bytes 42000808 | solution.py:102
  121.3 0.8 dynamic_slice.32
  122.7 1.1 constant_dynamic-slice_fusion.2
  124.3 0.8 compare_select_fusion.5
  125.0 4.7 %gather_fusion = bf16[512,512]{1,0:T(8,128)(2,1)S(1)} fusion(bf16[4160,512]{1,0:T(8,128)(2,1)} %get-tuple-element.426, s32[1024]{0:T(1024)S(1)} %pad_clamp_fusion.3), kind=kCustom, calls=%fused_computation.clone.clone.1 | custom fusion | bytes 1050624 | tf_op jit(solution)/shard_map/while/body/eval_jaxpr/gather | solution.py:81
  129.8 1.4 convolution_add_fusion.6
  131.2 0.8 dynamic_slice.33
  132.1 3.7 %fusion.73 = bf16[512,512]{1,0:T(8,128)(2,1)} fusion(bf16[2048,512]{1,0:T(8,128)(2,1)} %get-tuple-element.428, s32[512]{0:T(512)S(1)} %dynamic_slice.33), kind=kOutput, calls=%fused_computation.15.clone.1 | convolution fusion | flops 1075052544 | bytes 2623488 | tf_op jit(solution)/shard_map/while/body/eval_jaxpr/dot_general | solution.py:76
  135.8 2.4 fusion.74
  139.8 0.8 constant_dynamic-update-slice_fusion.2
  140.6 3.6 %select_add_fusion.2 = f32[2048,512]{1,0:T(8,128)} fusion(f32[2048,512]{1,0:T(8,128)} %get-tuple-element.396, s32[512]{0:T(512)S(1)} %dynamic_slice.33, pred[]{:T(512)S(6)} %compare.3, f32[512,512]{0,1:T(8,128)S(1)} %get-tuple-element.371, f32[512]{0:T(512)S(1)} %get-tuple-element.434, f32[512]{0:T(512)S(1)} %get-tuple-element.433, ...), kind=kOutput, calls=%fused_computation.8.clone.1 | convolution fusion | flops 1079508992 | bytes 9447937 | tf_op jit(solution)/shard_map/while/body/eval_jaxpr/dot_general | solution.py:94
  144.2 0.8 dynamic_slice.32
  145.6 1.1 constant_dynamic-slice_fusion.2
  147.9 4.7 %gather_fusion = bf16[512,512]{1,0:T(8,128)(2,1)S(1)} fusion(bf16[4160,512]{1,0:T(8,128)(2,1)} %get-tuple-element.426, s32[1024]{0:T(1024)S(1)} %pad_clamp_fusion.3), kind=kCustom, calls=%fused_computation.clone.clone.1 | custom fusion | bytes 1050624 | tf_op jit(solution)/shard_map/while/body/eval_jaxpr/gather | solution.py:81
  152.7 1.4 convolution_add_fusion.6
  154.1 0.8 dynamic_slice.33
  154.9 3.7 %fusion.73 = bf16[512,512]{1,0:T(8,128)(2,1)} fusion(bf16[2048,512]{1,0:T(8,128)(2,1)} %get-tuple-element.428, s32[512]{0:T(512)S(1)} %dynamic_slice.33), kind=kOutput, calls=%fused_computation.15.clone.1 | convolution fusion | flops 1075052544 | bytes 2623488 | tf_op jit(solution)/shard_map/while/body/eval_jaxpr/dot_general | solution.py:76
  158.6 2.4 fusion.74
  162.6 0.8 constant_dynamic-update-slice_fusion.2
  163.4 5.8 %select_add_fusion.2 = f32[2048,512]{1,0:T(8,128)} fusion(f32[2048,512]{1,0:T(8,128)} %get-tuple-element.396, s32[512]{0:T(512)S(1)} %dynamic_slice.33, pred[]{:T(512)S(6)} %compare.3, f32[512,512]{0,1:T(8,128)S(1)} %get-tuple-element.371, f32[512]{0:T(512)S(1)} %get-tuple-element.434, f32[512]{0:T(512)S(1)} %get-tuple-element.433, ...), kind=kOutput, calls=%fused_computation.8.clone.1 | convolution fusion | flops 1079508992 | bytes 9447937 | tf_op jit(solution)/shard_map/while/body/eval_jaxpr/dot_general | solution.py:94
  169.3 0.8 dynamic_slice.32
  170.7 1.1 constant_dynamic-slice_fusion.2
  172.3 0.8 compare_select_fusion.5
  173.0 4.7 %gather_fusion = bf16[512,512]{1,0:T(8,128)(2,1)S(1)} fusion(bf16[4160,512]{1,0:T(8,128)(2,1)} %get-tuple-element.426, s32[1024]{0:T(1024)S(1)} %pad_clamp_fusion.3), kind=kCustom, calls=%fused_computation.clone.clone.1 | custom fusion | bytes 1050624 | tf_op jit(solution)/shard_map/while/body/eval_jaxpr/gather | solution.py:81
  177.8 1.4 convolution_add_fusion.6
  179.2 0.8 dynamic_slice.33
  180.1 3.7 %fusion.73 = bf16[512,512]{1,0:T(8,128)(2,1)} fusion(bf16[2048,512]{1,0:T(8,128)(2,1)} %get-tuple-element.428, s32[512]{0:T(512)S(1)} %dynamic_slice.33), kind=kOutput, calls=%fused_computation.15.clone.1 | convolution fusion | flops 1075052544 | bytes 2623488 | tf_op jit(solution)/shard_map/while/body/eval_jaxpr/dot_general | solution.py:76
  183.8 2.4 fusion.74
  187.7 0.8 constant_dynamic-update-slice_fusion.2
  188.6 5.8 %select_add_fusion.2 = f32[2048,512]{1,0:T(8,128)} fusion(f32[2048,512]{1,0:T(8,128)} %get-tuple-element.396, s32[512]{0:T(512)S(1)} %dynamic_slice.33, pred[]{:T(512)S(6)} %compare.3, f32[512,512]{0,1:T(8,128)S(1)} %get-tuple-element.371, f32[512]{0:T(512)S(1)} %get-tuple-element.434, f32[512]{0:T(512)S(1)} %get-tuple-element.433, ...), kind=kOutput, calls=%fused_computation.8.clone.1 | convolution fusion | flops 1079508992 | bytes 9447937 | tf_op jit(solution)/shard_map/while/body/eval_jaxpr/dot_general | solution.py:94
  194.4 0.8 dynamic_slice.32
  195.9 1.1 constant_dynamic-slice_fusion.2
  198.2 4.7 %gather_fusion = bf16[512,512]{1,0:T(8,128)(2,1)S(1)} fusion(bf16[4160,512]{1,0:T(8,128)(2,1)} %get-tuple-element.426, s32[1024]{0:T(1024)S(1)} %pad_clamp_fusion.3), kind=kCustom, calls=%fused_computation.clone.clone.1 | custom fusion | bytes 1050624 | tf_op jit(solution)/shard_map/while/body/eval_jaxpr/gather | solution.py:81
  202.9 1.4 convolution_add_fusion.6
  204.3 0.8 dynamic_slice.33
  205.2 3.7 %fusion.73 = bf16[512,512]{1,0:T(8,128)(2,1)} fusion(bf16[2048,512]{1,0:T(8,128)(2,1)} %get-tuple-element.428, s32[512]{0:T(512)S(1)} %dynamic_slice.33), kind=kOutput, calls=%fused_computation.15.clone.1 | convolution fusion | flops 1075052544 | bytes 2623488 | tf_op jit(solution)/shard_map/while/body/eval_jaxpr/dot_general | solution.py:76
  208.9 2.4 fusion.74
  212.9 0.8 constant_dynamic-update-slice_fusion.2
  213.7 5.8 %select_add_fusion.2 = f32[2048,512]{1,0:T(8,128)} fusion(f32[2048,512]{1,0:T(8,128)} %get-tuple-element.396, s32[512]{0:T(512)S(1)} %dynamic_slice.33, pred[]{:T(512)S(6)} %compare.3, f32[512,512]{0,1:T(8,128)S(1)} %get-tuple-element.371, f32[512]{0:T(512)S(1)} %get-tuple-element.434, f32[512]{0:T(512)S(1)} %get-tuple-element.433, ...), kind=kOutput, calls=%fused_computation.8.clone.1 | convolution fusion | flops 1079508992 | bytes 9447937 | tf_op jit(solution)/shard_map/while/body/eval_jaxpr/dot_general | solution.py:94
  219.6 3.9 %convert_element_type.31 = bf16[2048,512]{1,0:T(8,128)(2,1)} convert(f32[2048,512]{1,0:T(8,128)} %get-tuple-element.100) | non-fusion elementwise | flops 1048576 | bytes 6291456 | tf_op jit(solution)/shard_map/convert_element_type | solution.py:109
  223.6 2.5 fusion.27
  226.0 25.4 %reduce-scatter.2.cloned.1.call-done = bf16[512,512]{1,0:T(8,128)(2,1)} async-done(((bf16[2048,512]{1,0:T(8,128)(2,1)}), bf16[512,512]{1,0:T(8,128)(2,1)}) %reduce-scatter.2.cloned.1.call-update) | async-done | bytes 524304 | tf_op jit(solution)/shard_map/reduce_scatter | solution.py:108
  251.4 3.5 %fusion.34 = (f32[512]{0:T(512)S(1)}, f32[512,512]{0,1:T(8,128)}) fusion(f32[512]{0:T(512)S(1)} %copy-done.15, bf16[512,512]{1,0:T(8,128)(2,1)S(1)} %copy-done, f32[512,512]{1,0:T(8,128)} %fusion.27, bf16[512,512]{1,0:T(8,128)(2,1)} %reduce-scatter.2.cloned.1.call-done, f32[512]{0:T(512)S(1)} %copy-done.16, bf16[1024,512]{1,0:T(8,128)(2,1)} %param.34), kind=kOutput, calls=%fused_computation.64 | convolution fusion | flops 539229696 | bytes 3676160 | tf_op jit(solution)/shard_map/dot_general | solution.py:124
  254.9 1.4 multiply_reduce_fusion.1
  256.3 1.5 add_convert_fusion.1
  257.9 11.2 %all_to_all.37 = bf16[512,4,128]{0,2,1:T(8,128)(2,1)S(1)} all-to-all(bf16[512,4,128]{0,2,1:T(8,128)(2,1)S(1)} %bitcast.52), channel_id=1, replica_groups=mesh['patch'=8,'hidden'=4] {'hidden'}, dimensions={1} | all-to-all | bytes 1048576 | tf_op jit(solution)/shard_map/all_to_all | solution.py:127
  269.1 1.0 copy.56
  (119 shorter events, 10.2 us)
Async XLA Ops:
  7.2 244.2 %copy-start = (bf16[512,512]{1,0:T(8,128)(2,1)S(1)}, bf16[512,512]{1,0:T(8,128)(2,1)}, u32[]{:S(2)}) copy-start(bf16[512,512]{1,0:T(8,128)(2,1)} %param.36) | copy-start | bytes 1572868
  7.2 28.3 %all-gather.2.cloned.1.call-start = ((), (), s32[]{:S(2)}) async-start(), calls=%async_computation.4 | async-start | bytes 2621440 | tf_op jit(solution)/shard_map/all_gather | solution.py:50
  46.5 12.0 %copy-start.10 = (s32[1,8,8]{2,1,0:T(8,128)S(1)}, s32[1,8,8]{2,1,0:T(8,128)}, u32[]{:S(2)}) copy-start(s32[1,8,8]{2,1,0:T(8,128)} %param.26) | copy-start | bytes 772
  46.5 57.7 %copy-start.7 = (bf16[1536,512]{1,0:T(8,128)(2,1)S(1)}, bf16[1536,512]{1,0:T(8,128)(2,1)}, u32[]{:S(2)}) copy-start(bf16[1536,512]{1,0:T(8,128)(2,1)} %param.28) | copy-start | bytes 4718596
  46.5 64.4 %collective-permute-start = (bf16[1024,512]{0,1:T(8,128)(2,1)}, bf16[1024,512]{0,1:T(8,128)(2,1)}, u32[]{:S(2)}, u32[]{:S(2)}) collective-permute-start(bf16[1024,512]{0,1:T(8,128)(2,1)} %copy.47), channel_id=1, source_target_pairs={{0,4},{4,8},{8,12},{12,16},{16,20},{20,24},{24,28},{28,0},{1,5},{5... | collective-permute-start | bytes 3145736 | tf_op jit(solution)/shard_map/ppermute | solution.py:15
  55.2 55.7 %collective-permute-start.1 = (bf16[1024,512]{0,1:T(8,128)(2,1)}, bf16[1024,512]{0,1:T(8,128)(2,1)}, u32[]{:S(2)}, u32[]{:S(2)}) collective-permute-start(bf16[1024,512]{0,1:T(8,128)(2,1)} %copy.49), channel_id=1, source_target_pairs={{4,0},{8,4},{12,8},{16,12},{20,16},{24,20},{28,24},{0,28},{5,1},{9... | collective-permute-start | bytes 3145736 | tf_op jit(solution)/shard_map/ppermute | solution.py:18
  100.6 10.2 %all-to-all-start.1 = ((bf16[8,8,512]{2,1,0:T(8,128)(2,1)}), bf16[8,8,512]{2,1,0:T(8,128)(2,1)S(1)}, u32[]{:S(2)}, u32[]{:S(2)}) async-start(bf16[8,8,512]{2,1,0:T(8,128)(2,1)} %bitcast.8), calls=%async_computation.1 | async-start | bytes 131072 | tf_op jit(solution)/shard_map/all_to_all | solution.py:57
  104.0 147.4 %reduce-scatter.2.cloned.1.call-start = ((), (), s32[]{:S(2)}) async-start(), calls=%async_computation.5 | async-start | bytes 2621440 | tf_op jit(solution)/shard_map/reduce_scatter | solution.py:108
  114.7 6.6 %copy-start.8 = (f32[512]{0:T(512)S(1)}, f32[512]{0:T(512)}, u32[]{:S(2)}) copy-start(f32[512]{0:T(512)} %param.32) | copy-start | bytes 6148
  114.7 6.6 %copy-start.9 = (f32[512]{0:T(512)S(1)}, f32[512]{0:T(512)}, u32[]{:S(2)}) copy-start(f32[512]{0:T(512)} %param.33) | copy-start | bytes 6148
  114.7 6.6 %copy-start.13 = (f32[512]{0:T(512)S(1)}, f32[512]{0:T(512)}, u32[]{:S(2)}) copy-start(f32[512]{0:T(512)} %param.29) | copy-start | bytes 6148
  114.7 6.6 %copy-start.14 = (f32[512]{0:T(512)S(1)}, f32[512]{0:T(512)}, u32[]{:S(2)}) copy-start(f32[512]{0:T(512)} %param.31) | copy-start | bytes 6148
  121.3 3.7 %copy-start.2 = (bf16[512,512]{1,0:T(8,128)(2,1)}, bf16[512,512]{1,0:T(8,128)(2,1)S(1)}, u32[]{:S(2)}) copy-start(bf16[512,512]{1,0:T(8,128)(2,1)S(1)} %get-tuple-element.424) | copy-start | bytes 1572868 | tf_op jit(solution)/shard_map/while
  121.3 8.5 %copy-start.4 = (bf16[512,512]{1,0:T(8,128)(2,1)}, bf16[512,512]{1,0:T(8,128)(2,1)S(1)}, u32[]{:S(2)}) copy-start(bf16[512,512]{1,0:T(8,128)(2,1)S(1)} %get-tuple-element.427) | copy-start | bytes 1572868 | tf_op jit(solution)/shard_map/while
  131.2 4.6 %copy-start.1 = (f32[512,512]{1,0:T(8,128)S(1)}, f32[512,512]{1,0:T(8,128)}, u32[]{:S(2)}) copy-start(f32[512,512]{1,0:T(8,128)} %convolution_add_fusion.6) | copy-start | bytes 3145732 | tf_op jit(solution)/shard_map/while
  140.6 3.6 %copy-start.3 = (bf16[512,512]{1,0:T(8,128)(2,1)S(1)}, bf16[512,512]{1,0:T(8,128)(2,1)}, u32[]{:S(2)}) copy-start(bf16[512,512]{1,0:T(8,128)(2,1)} %copy-done.2) | copy-start | bytes 1572868 | tf_op jit(solution)/shard_map/while
  140.6 3.6 %copy-start.5 = (bf16[512,512]{1,0:T(8,128)(2,1)S(1)}, bf16[512,512]{1,0:T(8,128)(2,1)}, u32[]{:S(2)}) copy-start(bf16[512,512]{1,0:T(8,128)(2,1)} %copy-done.4) | copy-start | bytes 1572868 | tf_op jit(solution)/shard_map/while
  144.2 3.7 %copy-start.2 = (bf16[512,512]{1,0:T(8,128)(2,1)}, bf16[512,512]{1,0:T(8,128)(2,1)S(1)}, u32[]{:S(2)}) copy-start(bf16[512,512]{1,0:T(8,128)(2,1)S(1)} %get-tuple-element.424) | copy-start | bytes 1572868 | tf_op jit(solution)/shard_map/while
  144.2 8.5 %copy-start.4 = (bf16[512,512]{1,0:T(8,128)(2,1)}, bf16[512,512]{1,0:T(8,128)(2,1)S(1)}, u32[]{:S(2)}) copy-start(bf16[512,512]{1,0:T(8,128)(2,1)S(1)} %get-tuple-element.427) | copy-start | bytes 1572868 | tf_op jit(solution)/shard_map/while
  154.1 4.6 %copy-start.1 = (f32[512,512]{1,0:T(8,128)S(1)}, f32[512,512]{1,0:T(8,128)}, u32[]{:S(2)}) copy-start(f32[512,512]{1,0:T(8,128)} %convolution_add_fusion.6) | copy-start | bytes 3145732 | tf_op jit(solution)/shard_map/while
  163.4 5.8 %copy-start.3 = (bf16[512,512]{1,0:T(8,128)(2,1)S(1)}, bf16[512,512]{1,0:T(8,128)(2,1)}, u32[]{:S(2)}) copy-start(bf16[512,512]{1,0:T(8,128)(2,1)} %copy-done.2) | copy-start | bytes 1572868 | tf_op jit(solution)/shard_map/while
  163.4 5.8 %copy-start.5 = (bf16[512,512]{1,0:T(8,128)(2,1)S(1)}, bf16[512,512]{1,0:T(8,128)(2,1)}, u32[]{:S(2)}) copy-start(bf16[512,512]{1,0:T(8,128)(2,1)} %copy-done.4) | copy-start | bytes 1572868 | tf_op jit(solution)/shard_map/while
  169.3 3.7 %copy-start.2 = (bf16[512,512]{1,0:T(8,128)(2,1)}, bf16[512,512]{1,0:T(8,128)(2,1)S(1)}, u32[]{:S(2)}) copy-start(bf16[512,512]{1,0:T(8,128)(2,1)S(1)} %get-tuple-element.424) | copy-start | bytes 1572868 | tf_op jit(solution)/shard_map/while
  169.3 8.5 %copy-start.4 = (bf16[512,512]{1,0:T(8,128)(2,1)}, bf16[512,512]{1,0:T(8,128)(2,1)S(1)}, u32[]{:S(2)}) copy-start(bf16[512,512]{1,0:T(8,128)(2,1)S(1)} %get-tuple-element.427) | copy-start | bytes 1572868 | tf_op jit(solution)/shard_map/while
  179.2 4.6 %copy-start.1 = (f32[512,512]{1,0:T(8,128)S(1)}, f32[512,512]{1,0:T(8,128)}, u32[]{:S(2)}) copy-start(f32[512,512]{1,0:T(8,128)} %convolution_add_fusion.6) | copy-start | bytes 3145732 | tf_op jit(solution)/shard_map/while
  188.6 5.8 %copy-start.3 = (bf16[512,512]{1,0:T(8,128)(2,1)S(1)}, bf16[512,512]{1,0:T(8,128)(2,1)}, u32[]{:S(2)}) copy-start(bf16[512,512]{1,0:T(8,128)(2,1)} %copy-done.2) | copy-start | bytes 1572868 | tf_op jit(solution)/shard_map/while
  188.6 5.8 %copy-start.5 = (bf16[512,512]{1,0:T(8,128)(2,1)S(1)}, bf16[512,512]{1,0:T(8,128)(2,1)}, u32[]{:S(2)}) copy-start(bf16[512,512]{1,0:T(8,128)(2,1)} %copy-done.4) | copy-start | bytes 1572868 | tf_op jit(solution)/shard_map/while
  194.4 3.7 %copy-start.2 = (bf16[512,512]{1,0:T(8,128)(2,1)}, bf16[512,512]{1,0:T(8,128)(2,1)S(1)}, u32[]{:S(2)}) copy-start(bf16[512,512]{1,0:T(8,128)(2,1)S(1)} %get-tuple-element.424) | copy-start | bytes 1572868 | tf_op jit(solution)/shard_map/while
  194.4 8.5 %copy-start.4 = (bf16[512,512]{1,0:T(8,128)(2,1)}, bf16[512,512]{1,0:T(8,128)(2,1)S(1)}, u32[]{:S(2)}) copy-start(bf16[512,512]{1,0:T(8,128)(2,1)S(1)} %get-tuple-element.427) | copy-start | bytes 1572868 | tf_op jit(solution)/shard_map/while
  204.3 4.5 %copy-start.1 = (f32[512,512]{1,0:T(8,128)S(1)}, f32[512,512]{1,0:T(8,128)}, u32[]{:S(2)}) copy-start(f32[512,512]{1,0:T(8,128)} %convolution_add_fusion.6) | copy-start | bytes 3145732 | tf_op jit(solution)/shard_map/while
  213.7 5.8 %copy-start.3 = (bf16[512,512]{1,0:T(8,128)(2,1)S(1)}, bf16[512,512]{1,0:T(8,128)(2,1)}, u32[]{:S(2)}) copy-start(bf16[512,512]{1,0:T(8,128)(2,1)} %copy-done.2) | copy-start | bytes 1572868 | tf_op jit(solution)/shard_map/while
  213.7 5.8 %copy-start.5 = (bf16[512,512]{1,0:T(8,128)(2,1)S(1)}, bf16[512,512]{1,0:T(8,128)(2,1)}, u32[]{:S(2)}) copy-start(bf16[512,512]{1,0:T(8,128)(2,1)} %copy-done.4) | copy-start | bytes 1572868 | tf_op jit(solution)/shard_map/while
  219.5 4.0 %copy-start.6 = (bf16[2048,512]{0,1:T(8,128)(2,1)S(1)}, bf16[2048,512]{0,1:T(8,128)(2,1)}, u32[]{:S(2)}) copy-start(bf16[2048,512]{0,1:T(8,128)(2,1)} %all-gather.2.cloned.1.call-done) | copy-start | bytes 6291460
  219.6 31.9 %copy-start.15 = (f32[512]{0:T(512)S(1)}, f32[512]{0:T(512)}, u32[]{:S(2)}) copy-start(f32[512]{0:T(512)} %param.37) | copy-start | bytes 6148
  219.6 31.8 %copy-start.16 = (f32[512]{0:T(512)S(1)}, f32[512]{0:T(512)}, u32[]{:S(2)}) copy-start(f32[512]{0:T(512)} %param.35) | copy-start | bytes 6148
  226.0 30.3 %copy-start.11 = (f32[512]{0:T(512)S(1)}, f32[512]{0:T(512)}, u32[]{:S(2)}) copy-start(f32[512]{0:T(512)} %param.39) | copy-start | bytes 6148
  226.0 30.3 %copy-start.12 = (f32[512]{0:T(512)S(1)}, f32[512]{0:T(512)}, u32[]{:S(2)}) copy-start(f32[512]{0:T(512)} %param.38) | copy-start | bytes 6148
Sparse Core Ops, SparseCore 0:
  10.1 25.2 all-gather.1
  223.7 27.6 reduce-scatter.1
where the time goes:
time: 279 us; the launch traced here: 277 us
  local copies, waits for them, and re-layouts  67.3 us (24%)
  matrix products  58.8 us (21%)
  waiting for transfers between devices  56.4 us (20%)
  blocking collectives  50 us (18%)
  other arithmetic  19 us (7%)
  between operations  14.2 us (5%)
  starting transfers between devices  8.36 us (3%)
  loops' own time  2.83 us (1%)
    all_to_all x1, blocking collectives, local(): lax.all_to_all(coarse_rows[0], 'patch', split_axis=0, concat_axis=0, tile...  38.8 us
    reduce_scatter x1, waiting for transfers between devices, local(): lax.psum_scatter(summed.astype(jnp.bfloat16), 'hidden', scatter_dimension...  25.4 us
    all_gather x1, waiting for transfers between devices, local(): own_block = lax.all_gather(nodes, 'hidden', axis=1, tiled=True)  25.3 us
    dot_general x4, matrix products, edge_block(): lax.dot_general(onehot, message.astype(jnp.bfloat16), (((0,), (0,)), ((),...  21.1 us
    gather x4, local copies, waits for them, and re-layouts, edge_block(): sender_table[sender_code]  19 us
    dot_general x4, matrix products, edge_block(): jnp.dot(onehot, own_block, preferred_element_type=jnp.float32)  14.8 us
    all_to_all x1, blocking collectives, local(): lax.all_to_all(new_rows, 'hidden', split_axis=1, concat_axis=0, tiled=True)  11.2 us
    dot_general x4, matrix products, edge_block(): jnp.dot(active, w_edge_out, preferred_element_type=jnp.float32) + b_edge_out  9.45 us
  transfers between devices with their start and end apart: 5, of which 3 were waited for; matrix products, arithmetic and copies ran while one was open for 5% of the time, Pallas kernels for 0%

commit v1 on v0

v1 whole, which is shorter than its diff:
```python
import functools

import jax
import jax.numpy as jnp
from jax import lax
from jax.experimental import pallas as pl
from jax.experimental.pallas import tpu as pltpu
from jax.sharding import PartitionSpec as P

layer_epsilon = 1e-05
MESH = pl.DeviceIdType.MESH
f32 = jnp.float32
bf16 = jnp.bfloat16


def normalize(output, norm_gain, norm_shift):
    row_mean = jnp.mean(output, axis=1, keepdims=True)
    centered = output - row_mean
    row_var = jnp.mean(jnp.square(centered), axis=1, keepdims=True)
    return centered * lax.rsqrt(row_var + layer_epsilon) * norm_gain + norm_shift


def silu(value):
    half = 0.5 * value
    return half + half * jnp.tanh(half)


def dot(a, b):
    return jnp.dot(a, b, preferred_element_type=f32)


def onehot_of(column, start, count):
    ids = lax.broadcasted_iota(jnp.int32, (column.shape[0], count), 1) + start
    return jnp.where(column == ids, 1.0, 0.0).astype(bf16)


def kernel(
    patches, slot, border, block,
    nodes, halo_col, coarse, live, recv_row, vecs,
    send_hbm, recv_hbm, edges_hbm, w_ei_hbm, w_eo_hbm, w_ni_hbm, w_no_hbm,
    nodes_out, edges_out,
    table, stage, req, rep, far_in, far_out, send_col, recv_col, edges,
    w_ei, w_eo, w_ni, w_no, pre, own_send, msg,
    give_far, got_far, give_cross, got_cross, give_near, got_near, fresh,
    load_sem, own_sem, store_sem, ag_send, ag_recv, halo_send, halo_recv,
    req_send, req_recv, rep_send, rep_recv, rs_send, rs_recv, out_send, out_recv,
):
    p = lax.axis_index("patch")
    h = lax.axis_index("hidden")
    near = h + 1 - 2 * lax.rem(h, 2)
    cross = lax.rem(h + 2, 4)
    diag = lax.rem(near + 2, 4)
    rows, cols = nodes.shape
    width = edges.shape[1]
    count = edges.shape[0]
    far = patches * slot
    after = lax.rem(p + 1, patches)
    before = lax.rem(p + patches - 1, patches)

    loads = [
        pltpu.make_async_copy(source, target, load_sem.at[i])
        for i, (source, target) in enumerate((
            (edges_hbm, edges), (recv_hbm, recv_col), (send_hbm, send_col),
            (w_ei_hbm, w_ei), (w_eo_hbm, w_eo), (w_ni_hbm, w_ni), (w_no_hbm, w_no),
        ))
    ]
    for load in loads:
        load.start()

    def mine(index):
        return pl.ds(pl.multiple_of(index * cols, cols), cols)

    barrier = pltpu.get_barrier_semaphore()
    for step in range(1, patches):
        pl.semaphore_signal(
            barrier, inc=1, device_id={"patch": lax.rem(p + step, patches)}, device_id_type=MESH
        )
    for peer in (near, cross, diag):
        pl.semaphore_signal(barrier, inc=1, device_id={"hidden": peer}, device_id_type=MESH)
    pl.semaphore_wait(barrier, patches - 1 + 3)

    def remote(source, target, s_sem, r_sem, device):
        return pltpu.make_async_remote_copy(
            src_ref=source, dst_ref=target, send_sem=s_sem, recv_sem=r_sem,
            device_id=device, device_id_type=MESH,
        )

    def slots(index):
        return pl.ds(pl.multiple_of(index * slot, slot), slot)

    asks = []
    for step in range(1, patches):
        owner = lax.rem(p + step, patches)
        ask = remote(
            coarse.at[slots(owner)], req.at[slots(p)],
            req_send.at[step - 1], req_recv.at[step - 1], {"patch": owner},
        )
        ask.start()
        asks.append(ask)

    half = rows // 2
    spans = [(0, half), (half, half), (rows, border), (rows + border, border), (rows + 2 * border, far)]

    def exchange(k, source):
        start, size = spans[k]
        span = pl.ds(start, size)
        pair = []
        for j, peer in ((1, cross), (0, near)):
            copy = remote(
                source, table.at[span, mine(h)], ag_send.at[k, j], ag_recv.at[k, j], {"hidden": peer}
            )
            copy.start()
            pair.append(copy)
        return pair

    def forward(k):
        start, size = spans[k]
        piece = table.at[pl.ds(start, size), mine(cross)]
        copy = remote(piece, piece, ag_send.at[k, 2], ag_recv.at[k, 2], {"hidden": near})
        copy.start()
        return copy

    pairs = [exchange(0, nodes.at[pl.ds(0, half)]), exchange(1, nodes.at[pl.ds(half, half)])]
    keep = pltpu.make_async_copy(nodes, table.at[pl.ds(0, rows), mine(h)], own_sem.at[0])
    keep.start()
    req[slots(p), :] = coarse[slots(p), :]
    pad = table.shape[0] - rows - 2 * border - far
    if pad:
        table[pl.ds(rows + 2 * border + far, pad), :] = jnp.zeros((pad, width), bf16)

    halos = []
    for side, target, start in ((1, after, rows), (0, before, rows + border)):
        part = pl.ds(side * border, border)
        picked = onehot_of(halo_col[part, :], 0, rows)
        stage[part, :] = dot(picked, nodes[...]).astype(bf16)
        copy = remote(
            stage.at[part], table.at[pl.ds(start, border), mine(h)],
            halo_send.at[side], halo_recv.at[side], {"patch": target},
        )
        copy.start()
        halos.append(copy)

    for ask in asks:
        ask.wait()
    rep[...] = dot(onehot_of(req[...][:, :1], 0, rows), nodes[...])
    answers = []
    for step in range(1, patches):
        reader = lax.rem(p + step, patches)
        answer = remote(
            rep.at[slots(reader)], far_in.at[slots(p)],
            rep_send.at[step - 1], rep_recv.at[step - 1], {"patch": reader},
        )
        answer.start()
        answers.append(answer)
    far_in[slots(p), :] = rep[slots(p), :]

    keep.wait()
    forwards = []
    for pair in pairs:
        pair[0].wait()
        forwards.append(forward(len(forwards)))
    for answer in answers:
        answer.wait()
    far_out[...] = far_in[...].astype(bf16)
    for i, copy in enumerate(halos):
        copy.wait()
        start, size = spans[2 + i]
        pairs.append(exchange(2 + i, table.at[pl.ds(start, size), mine(h)]))
    pairs.append(exchange(4, far_out))
    keep = pltpu.make_async_copy(
        far_out, table.at[pl.ds(rows + 2 * border, far), mine(h)], own_sem.at[1]
    )
    keep.start()
    for i in range(2):
        pairs[i][1].wait()
        forwards[i].wait()
    for load in loads[:4]:
        load.wait()

    def first(step, carry):
        part = pl.ds(pl.multiple_of(step * block, block), block)
        receiver_rows = dot(onehot_of(recv_col[part, :], 0, rows), table[pl.ds(0, rows), :]).astype(bf16)
        own_send[part, :] = dot(
            onehot_of(send_col[part, :], 0, rows), table[pl.ds(0, rows), :]
        ).astype(bf16)
        pre[part, :] = (
            dot(edges[part, :], w_ei[pl.ds(0, width), :])
            + dot(receiver_rows, w_ei[pl.ds(2 * width, width), :])
            + vecs[0:1, :]
        )
        return carry

    lax.fori_loop(0, count // block, first, 0)

    keep.wait()
    for k in (2, 3, 4):
        pairs[k][0].wait()
        forwards.append(forward(k))
    for k in (2, 3, 4):
        pairs[k][1].wait()
        forwards[k].wait()
    for load in loads[4:]:
        load.wait()
    rest = table.shape[0] - rows

    def second(step, carry):
        part = pl.ds(pl.multiple_of(step * block, block), block)
        other = dot(onehot_of(send_col[part, :], rows, rest), table[pl.ds(rows, rest), :])
        sender_rows = (other + own_send[part, :].astype(f32)).astype(bf16)
        active = silu(pre[part, :] + dot(sender_rows, w_ei[pl.ds(width, width), :])).astype(bf16)
        output = dot(active, w_eo[...]) + vecs[1:2, :]
        update = normalize(output, vecs[2:3, :], vecs[3:4, :])
        position = lax.broadcasted_iota(jnp.int32, (block, 1), 0) + step * block
        message = jnp.where(position < live[...], update, 0.0)
        msg[part, :] = message.astype(bf16)
        edges[part, :] = (edges[part, :].astype(f32) + message).astype(bf16)
        return carry

    lax.fori_loop(0, count // block, second, 0)
    save = pltpu.make_async_copy(edges, edges_out, store_sem.at[0])
    save.start()

    share = rows // 4

    def sums(owner):
        ids = lax.broadcasted_iota(jnp.int32, (share, count), 0) + owner * share
        return dot(jnp.where(recv_row[...] == ids, 1.0, 0.0).astype(bf16), msg[...])

    give_far[...] = sums(diag).astype(bf16)
    to_far = remote(give_far, got_far, rs_send.at[0], rs_recv.at[0], {"hidden": near})
    to_far.start()
    pre[pl.ds(0, share), :] = sums(cross)
    to_far.wait()
    cut = share // 2
    to_cross = []
    for i in range(2):
        part = pl.ds(i * cut, cut)
        give_cross[part, :] = (pre[part, :] + got_far[part, :].astype(f32)).astype(bf16)
        copy = remote(
            give_cross.at[part], got_cross.at[part], rs_send.at[1 + i], rs_recv.at[1 + i], {"hidden": cross}
        )
        copy.start()
        to_cross.append(copy)
    give_near[...] = sums(near).astype(bf16)
    to_near = remote(give_near, got_near, rs_send.at[3], rs_recv.at[3], {"hidden": near})
    to_near.start()
    pre[pl.ds(0, share), :] = sums(h)
    own_rows = pl.ds(pl.multiple_of(h * share, share), share)
    pre[pl.ds(share, share), :] = (
        dot(table[own_rows, :], w_ni[pl.ds(0, width), :]) + vecs[4:5, :]
    )
    to_near.wait()
    outs = []
    for i in range(2):
        part = pl.ds(i * cut, cut)
        to_cross[i].wait()
        total = pre[part, :] + got_near[part, :].astype(f32) + got_cross[part, :].astype(f32)
        node_pre = pre[pl.ds(share + i * cut, cut), :] + dot(
            total.astype(bf16), w_ni[pl.ds(width, width), :]
        )
        output = dot(silu(node_pre).astype(bf16), w_no[...]) + vecs[5:6, :]
        update = normalize(output, vecs[6:7, :], vecs[7:8, :])
        place = pl.ds(pl.multiple_of(h * share + i * cut, cut), cut)
        fresh[part, :] = (table[place, :].astype(f32) + update).astype(bf16)
        for j, peer in enumerate((cross, diag, near)):
            copy = remote(
                fresh.at[part, mine(peer)], nodes_out.at[place, :],
                out_send.at[i, j], out_recv.at[i, j], {"hidden": peer},
            )
            copy.start()
            outs.append(copy)
        nodes_out[place, :] = fresh[part, mine(h)]
    for copy in outs:
        copy.wait()
    save.wait()


def local(
    nodes, edges, senders, receivers, halo_rows, coarse_rows, edge_count,
    w_edge_in, b_edge_in, w_edge_out, b_edge_out, edge_gain, edge_shift,
    w_node_in, b_node_in, w_node_out, b_node_out, node_gain, node_shift,
    *, patches,
):
    rows, cols = nodes.shape
    count, width = edges.shape
    border = halo_rows.shape[2]
    slot = coarse_rows.shape[2]
    far = patches * slot
    table_rows = -(-(rows + 2 * border + far) // 256) * 256
    share = rows // 4
    block = min(512, count)
    vecs = jnp.stack([
        b_edge_in, b_edge_out, edge_gain, edge_shift, b_node_in, b_node_out, node_gain, node_shift
    ])
    coarse = jnp.broadcast_to(coarse_rows.reshape(far, 1), (far, 128))
    vmem = pl.BlockSpec(memory_space=pltpu.VMEM)
    hbm = pl.BlockSpec(memory_space=pl.ANY)
    dma = pltpu.SemaphoreType.DMA
    return pl.pallas_call(
        functools.partial(kernel, patches, slot, border, block),
        out_shape=(
            jax.ShapeDtypeStruct((rows, cols), bf16),
            jax.ShapeDtypeStruct((count, width), bf16),
        ),
        in_specs=[vmem] * 6 + [hbm] * 7,
        out_specs=(vmem, hbm),
        scratch_shapes=[
            pltpu.VMEM((table_rows, width), bf16),
            pltpu.VMEM((2 * border, cols), bf16),
            pltpu.VMEM((far, 128), jnp.int32),
            pltpu.VMEM((far, cols), f32),
            pltpu.VMEM((far, cols), f32),
            pltpu.VMEM((far, cols), bf16),
            pltpu.VMEM((count, 1), jnp.int32),
            pltpu.VMEM((count, 1), jnp.int32),
            pltpu.VMEM((count, width), bf16),
            pltpu.VMEM(w_edge_in.shape, bf16),
            pltpu.VMEM(w_edge_out.shape, bf16),
            pltpu.VMEM(w_node_in.shape, bf16),
            pltpu.VMEM(w_node_out.shape, bf16),
            pltpu.VMEM((count, width), f32),
            pltpu.VMEM((count, width), bf16),
            pltpu.VMEM((count, width), bf16),
        ] + [pltpu.VMEM((share, width), bf16)] * 7 + [
            dma((7,)), dma((2,)), dma((1,)), dma((5, 3)), dma((5, 3)), dma((2,)), dma((2,)),
            dma((patches - 1,)), dma((patches - 1,)), dma((patches - 1,)), dma((patches - 1,)),
            dma((4,)), dma((4,)), dma((2, 3)), dma((2, 3)),
        ],
        compiler_params=pltpu.CompilerParams(
            collective_id=0, has_side_effects=True, vmem_limit_bytes=60 * 1024 * 1024
        ),
    )(
        nodes, halo_rows.reshape(-1, 1), coarse, edge_count.reshape(1, 1),
        receivers.reshape(1, -1), vecs,
        senders.reshape(-1, 1), receivers.reshape(-1, 1), edges,
        w_edge_in, w_edge_out, w_node_in, w_node_out,
    )


def solution(mesh):
    spread = P(("patch", "hidden"))
    return jax.shard_map(
        functools.partial(local, patches=mesh.shape["patch"]),
        mesh=mesh,
        in_specs=(
            P("patch", "hidden"), P(("patch", "hidden"), None), spread, spread,
            P("patch", None, None), P("patch", None, None), spread,
        ) + (P(),) * 12,
        out_specs=(P("patch", "hidden"), P(("patch", "hidden"), None)),
        check_vma=False,
    )
```

time: 279 us -> 86.1 us (0.31)
  Pallas kernels: 0 us -> 71.2 us
  matrix products: 58.8 us -> 0 us
  waiting for transfers between devices: 56.4 us -> 0 us
  local copies, waits for them, and re-layouts: 67.3 us -> 13.3 us
  blocking collectives: 50 us -> 0 us
  other arithmetic: 19 us -> 0 us
  between operations: 14.2 us -> 1.31 us
  starting transfers between devices: 8.36 us -> 0 us
  loops' own time: 2.83 us -> 0 us
    pallas_call x0 -> x1, Pallas kernels: none -> 71.2 us  [local(): pl.pallas_call(functools.partial(kernel, patches, slot, border, block), o...]
    dot_general x22 -> x0, matrix products: 58.8 us -> none  [the longest x4 21.1 us: edge_block(): lax.dot_general(onehot, message.astype(jnp.bfloat16), (((0,), (0,)), ((),...]
    all_to_all x2 -> x0, blocking collectives: 50 us -> none  [the longest x1 38.8 us: local(): lax.all_to_all(coarse_rows[0], 'patch', split_axis=0, concat_axis=0, tile...]
    gather x9 -> x0, local copies, waits for them, and re-layouts: 36.5 us -> none  [the longest x4 19 us: edge_block(): sender_table[sender_code]]
    reduce_scatter x1 -> x0, waiting for transfers between devices: 25.4 us -> none  [local(): lax.psum_scatter(summed.astype(jnp.bfloat16), 'hidden', scatter_dimension...]
    all_gather x1 -> x0, waiting for transfers between devices: 25.3 us -> none  [local(): own_block = lax.all_gather(nodes, 'hidden', axis=1, tiled=True)]
    dynamic_slice x16 -> x0, local copies, waits for them, and re-layouts: 11.8 us -> none  [the longest x8 5.18 us: edge_block(): latent = lax.dynamic_slice_in_dim(edges, offset, block_rows, 0)]
    all_to_all x1 -> x0, waiting for transfers between devices: 5.7 us -> none  [local(): lax.all_to_all(own_block[requested], 'patch', split_axis=0, concat_axis=0...]
  transfers between devices with their start and end apart: 5 -> 0, of which waited for: 3 -> 0; matrix products, arithmetic and copies ran while one was open for 5% -> 0% of each run, Pallas kernels for 0% -> 0%
where the time goes in v1:
time: 86.1 us; the launch traced here: 85.7 us
  Pallas kernels  71.2 us (83%)
  local copies, waits for them, and re-layouts  13.3 us (15%)
  between operations  1.31 us (2%)
    pallas_call x1, Pallas kernels, local(): pl.pallas_call(functools.partial(kernel, patches, slot, border, block), o...  71.2 us
    unnamed x6, local copies, waits for them, and re-layouts  6.97 us
    reshape x1, local copies, waits for them, and re-layouts, local(): senders.reshape(-1, 1)  2.05 us

profile of v1, /device:TPU:0, one launch (start us, length us, event | category | flops | bytes accessed | tf_op | source)
XLA Modules:
  0.0 85.7 jit_solution(4835218261086561605)
XLA Ops:
  0.6 0.0 copy-start
  1.3 0.8 broadcast_in_dim.7
  2.1 0.7 copy.24
  2.8 1.4 %stack.35.vecs = f32[8,512]{1,0:T(8,128)} concatenate(f32[1,512]{1,0:T(1,128)} %bitcast.22, f32[1,512]{1,0:T(1,128)} %bitcast.23, f32[1,512]{1,0:T(1,128)} %bitcast.24, f32[1,512]{1,0:T(1,128)} %bitcast.25, f32[1,512]{1,0:T(1,128)} %bitcast.26, f32[1,512]{1,0:T(1,128)} %bitcast.27, f32[1,512]{1,0:T(1,128)} %bitcast.28, f32[1,512]{1,0:T(1,128)} %bitcast.29), dimensions={0} | concatenate | bytes 32768 | tf_op jit(solution)/shard_map/stack | solution.py:292
  4.2 0.7 broadcast_in_dim.8.coarse
  4.9 1.3 %copy.25 = s32[1,2048]{0,1:T(8,128)} copy(s32[1,2048]{1,0:T(1,128)S(1)} %bitcast.17) | data formatting | bytes 16384
  6.2 2.1 %copy.22.send_hbm = s32[2048,1]{1,0:T(8,128)} copy(s32[2048,1]{0,1:T(1,128)} %bitcast.20) | data formatting | bytes 16384 | tf_op jit(solution)/shard_map/reshape | solution.py:335
  8.3 0.0 copy-done
  8.3 1.4 %copy.23.recv_hbm = s32[2048,1]{1,0:T(8,128)} copy(s32[2048,1]{0,1:T(1,128)S(1)} %bitcast.19) | data formatting | bytes 16384 | tf_op jit(solution)/shard_map/reshape | solution.py:335
  9.7 71.2 %shard_map.194 = (bf16[2048,128]{1,0:T(8,128)(2,1)}, bf16[2048,512]{1,0:T(8,128)(2,1)}) custom-call(bf16[2048,128]{1,0:T(8,128)(2,1)} %nodes.1, s32[2048,1]{1,0:T(8,128)} %bitcast.16, s32[64,128]{1,0:T(8,128)} %broadcast_in_dim.8.coarse, s32[1,1]{1,0:T(1,128)} %bitcast.15.live, s32[1,2048]{1,0:T(1,128)} %bitcast.18, f32[8,512]{1,0:T(8,128)} %stack.35.vecs, ...), custom_call_target="tpu_custom_call" | custom-call | tf_op jit(solution)/shard_map/pallas_call | solution.py:299
  80.8 1.9 %copy.29 = bf16[2048,128]{1,0:T(8,128)(2,1)} copy(bf16[2048,128]{1,0:T(8,128)(2,1)} %get-tuple-element.4) | data formatting | bytes 1048576
  82.7 3.0 %copy.30 = bf16[2048,512]{1,0:T(8,128)(2,1)} copy(bf16[2048,512]{1,0:T(8,128)(2,1)} %get-tuple-element.5) | data formatting | bytes 4194304
Async XLA Ops:
  0.6 7.7 %copy-start = (s32[2048]{0:T(1024)S(1)}, s32[2048]{0:T(1024)}, u32[]{:S(2)}) copy-start(s32[2048]{0:T(1024)} %param.22) | copy-start | bytes 24580

commit v2 on v1

--- a/solution.py
+++ b/solution.py
@@ -29,6 +29,10 @@
     return jnp.dot(a, b, preferred_element_type=f32)
 
 
+def column_of(row):
+    return jnp.transpose(jnp.broadcast_to(row, (128, row.shape[1])))[:, :1]
+
+
 def onehot_of(column, start, count):
     ids = lax.broadcasted_iota(jnp.int32, (column.shape[0], count), 1) + start
     return jnp.where(column == ids, 1.0, 0.0).astype(bf16)
@@ -36,8 +40,9 @@
 
 def kernel(
     patches, slot, border, block,
-    nodes, halo_col, coarse, live, recv_row, vecs,
-    send_hbm, recv_hbm, edges_hbm, w_ei_hbm, w_eo_hbm, w_ni_hbm, w_no_hbm,
+    nodes, halo, coarse, live, send_row, recv_row,
+    b_ei, b_eo, e_gain, e_shift, b_ni, b_no, n_gain, n_shift,
+    edges_hbm, w_ei_hbm, w_eo_hbm, w_ni_hbm, w_no_hbm,
     nodes_out, edges_out,
     table, stage, req, rep, far_in, far_out, send_col, recv_col, edges,
     w_ei, w_eo, w_ni, w_no, pre, own_send, msg,
@@ -60,8 +65,8 @@
     loads = [
         pltpu.make_async_copy(source, target, load_sem.at[i])
         for i, (source, target) in enumerate((
-            (edges_hbm, edges), (recv_hbm, recv_col), (send_hbm, send_col),
-            (w_ei_hbm, w_ei), (w_eo_hbm, w_eo), (w_ni_hbm, w_ni), (w_no_hbm, w_no),
+            (edges_hbm, edges), (w_ei_hbm, w_ei), (w_eo_hbm, w_eo), (w_ni_hbm, w_ni),
+            (w_no_hbm, w_no),
         ))
     ]
     for load in loads:
@@ -99,7 +104,12 @@
         asks.append(ask)
 
     half = rows // 2
-    spans = [(0, half), (half, half), (rows, border), (rows + border, border), (rows + 2 * border, far)]
+    piece_rows = border // 2
+    spans = [(0, half), (half, half)]
+    for i in range(2):
+        spans.append((rows + i * piece_rows, piece_rows))
+        spans.append((rows + border + i * piece_rows, piece_rows))
+    spans.append((rows + 2 * border, far))
 
     def exchange(k, source):
         start, size = spans[k]
@@ -129,16 +139,19 @@
         table[pl.ds(rows + 2 * border + far, pad), :] = jnp.zeros((pad, width), bf16)
 
     halos = []
-    for side, target, start in ((1, after, rows), (0, before, rows + border)):
-        part = pl.ds(side * border, border)
-        picked = onehot_of(halo_col[part, :], 0, rows)
-        stage[part, :] = dot(picked, nodes[...]).astype(bf16)
-        copy = remote(
-            stage.at[part], table.at[pl.ds(start, border), mine(h)],
-            halo_send.at[side], halo_recv.at[side], {"patch": target},
-        )
-        copy.start()
-        halos.append(copy)
+    for i in range(2):
+        for side, target in ((1, after), (0, before)):
+            k = len(halos)
+            start, size = spans[2 + k]
+            held = pl.ds(k * piece_rows, piece_rows)
+            ids = column_of(halo[side : side + 1, i * piece_rows : (i + 1) * piece_rows])
+            stage[held, :] = dot(onehot_of(ids, 0, rows), nodes[...]).astype(bf16)
+            copy = remote(
+                stage.at[held], table.at[pl.ds(start, size), mine(h)],
+                halo_send.at[k], halo_recv.at[k], {"patch": target},
+            )
+            copy.start()
+            halos.append(copy)
 
     for ask in asks:
         ask.wait()
@@ -155,18 +168,34 @@
     far_in[slots(p), :] = rep[slots(p), :]
 
     keep.wait()
-    forwards = []
-    for pair in pairs:
-        pair[0].wait()
-        forwards.append(forward(len(forwards)))
+    recv_col[...] = column_of(recv_row[...])
+    send_col[...] = column_of(send_row[...])
+    for load in loads[:2]:
+        load.wait()
+
+    def begin(step, carry):
+        part = pl.ds(pl.multiple_of(step * block, block), block)
+        pre[part, :] = dot(edges[part, :], w_ei[pl.ds(0, width), :]) + b_ei[...]
+        return carry
+
+    lax.fori_loop(0, count // block, begin, 0)
+
+    def relay(k):
+        halos[k].wait()
+        start, size = spans[2 + k]
+        pairs.append(exchange(2 + k, table.at[pl.ds(start, size), mine(h)]))
+
+    relay(0)
+    relay(1)
+    pairs[0][0].wait()
+    forwards = [forward(0)]
+    relay(2)
+    pairs[1][0].wait()
+    forwards.append(forward(1))
     for answer in answers:
         answer.wait()
     far_out[...] = far_in[...].astype(bf16)
-    for i, copy in enumerate(halos):
-        copy.wait()
-        start, size = spans[2 + i]
-        pairs.append(exchange(2 + i, table.at[pl.ds(start, size), mine(h)]))
-    pairs.append(exchange(4, far_out))
+    far_pair = exchange(6, far_out)
     keep = pltpu.make_async_copy(
         far_out, table.at[pl.ds(rows + 2 * border, far), mine(h)], own_sem.at[1]
     )
@@ -174,8 +203,6 @@
     for i in range(2):
         pairs[i][1].wait()
         forwards[i].wait()
-    for load in loads[:4]:
-        load.wait()
 
     def first(step, carry):
         part = pl.ds(pl.multiple_of(step * block, block), block)
@@ -183,23 +210,28 @@
         own_send[part, :] = dot(
             onehot_of(send_col[part, :], 0, rows), table[pl.ds(0, rows), :]
         ).astype(bf16)
-        pre[part, :] = (
-            dot(edges[part, :], w_ei[pl.ds(0, width), :])
-            + dot(receiver_rows, w_ei[pl.ds(2 * width, width), :])
-            + vecs[0:1, :]
-        )
+        pre[part, :] = pre[part, :] + dot(receiver_rows, w_ei[pl.ds(2 * width, width), :])
         return carry
 
-    lax.fori_loop(0, count // block, first, 0)
-
-    keep.wait()
+    steps = count // block
+    lax.fori_loop(0, 1, first, 0)
+    relay(3)
+    pairs.append(far_pair)
+    lax.fori_loop(1, steps - 1, first, 0)
     for k in (2, 3, 4):
         pairs[k][0].wait()
         forwards.append(forward(k))
-    for k in (2, 3, 4):
+    lax.fori_loop(steps - 1, steps, first, 0)
+
+    keep.wait()
+    for k in (6, 5):
+        pairs[k][0].wait()
+        forwards.append(forward(k))
+    for k in range(2, 7):
         pairs[k][1].wait()
-        forwards[k].wait()
-    for load in loads[4:]:
+    for copy in forwards[2:]:
+        copy.wait()
+    for load in loads[2:]:
         load.wait()
     rest = table.shape[0] - rows
 
@@ -208,8 +240,8 @@
         other = dot(onehot_of(send_col[part, :], rows, rest), table[pl.ds(rows, rest), :])
         sender_rows = (other + own_send[part, :].astype(f32)).astype(bf16)
         active = silu(pre[part, :] + dot(sender_rows, w_ei[pl.ds(width, width), :])).astype(bf16)
-        output = dot(active, w_eo[...]) + vecs[1:2, :]
-        update = normalize(output, vecs[2:3, :], vecs[3:4, :])
+        output = dot(active, w_eo[...]) + b_eo[...]
+        update = normalize(output, e_gain[...], e_shift[...])
         position = lax.broadcasted_iota(jnp.int32, (block, 1), 0) + step * block
         message = jnp.where(position < live[...], update, 0.0)
         msg[part, :] = message.astype(bf16)
@@ -231,9 +263,9 @@
     to_far.start()
     pre[pl.ds(0, share), :] = sums(cross)
     to_far.wait()
-    cut = share // 2
+    cut = share // 4
     to_cross = []
-    for i in range(2):
+    for i in range(4):
         part = pl.ds(i * cut, cut)
         give_cross[part, :] = (pre[part, :] + got_far[part, :].astype(f32)).astype(bf16)
         copy = remote(
@@ -242,24 +274,24 @@
         copy.start()
         to_cross.append(copy)
     give_near[...] = sums(near).astype(bf16)
-    to_near = remote(give_near, got_near, rs_send.at[3], rs_recv.at[3], {"hidden": near})
+    to_near = remote(give_near, got_near, rs_send.at[5], rs_recv.at[5], {"hidden": near})
     to_near.start()
     pre[pl.ds(0, share), :] = sums(h)
     own_rows = pl.ds(pl.multiple_of(h * share, share), share)
     pre[pl.ds(share, share), :] = (
-        dot(table[own_rows, :], w_ni[pl.ds(0, width), :]) + vecs[4:5, :]
+        dot(table[own_rows, :], w_ni[pl.ds(0, width), :]) + b_ni[...]
     )
     to_near.wait()
     outs = []
-    for i in range(2):
+    for i in range(4):
         part = pl.ds(i * cut, cut)
         to_cross[i].wait()
         total = pre[part, :] + got_near[part, :].astype(f32) + got_cross[part, :].astype(f32)
         node_pre = pre[pl.ds(share + i * cut, cut), :] + dot(
             total.astype(bf16), w_ni[pl.ds(width, width), :]
         )
-        output = dot(silu(node_pre).astype(bf16), w_no[...]) + vecs[5:6, :]
-        update = normalize(output, vecs[6:7, :], vecs[7:8, :])
+        output = dot(silu(node_pre).astype(bf16), w_no[...]) + b_no[...]
+        update = normalize(output, n_gain[...], n_shift[...])
         place = pl.ds(pl.multiple_of(h * share + i * cut, cut), cut)
         fresh[part, :] = (table[place, :].astype(f32) + update).astype(bf16)
         for j, peer in enumerate((cross, diag, near)):
@@ -289,9 +321,6 @@
     table_rows = -(-(rows + 2 * border + far) // 256) * 256
     share = rows // 4
     block = min(512, count)
-    vecs = jnp.stack([
-        b_edge_in, b_edge_out, edge_gain, edge_shift, b_node_in, b_node_out, node_gain, node_shift
-    ])
     coarse = jnp.broadcast_to(coarse_rows.reshape(far, 1), (far, 128))
     vmem = pl.BlockSpec(memory_space=pltpu.VMEM)
     hbm = pl.BlockSpec(memory_space=pl.ANY)
@@ -302,7 +331,7 @@
             jax.ShapeDtypeStruct((rows, cols), bf16),
             jax.ShapeDtypeStruct((count, width), bf16),
         ),
-        in_specs=[vmem] * 6 + [hbm] * 7,
+        in_specs=[vmem] * 14 + [hbm] * 5,
         out_specs=(vmem, hbm),
         scratch_shapes=[
             pltpu.VMEM((table_rows, width), bf16),
@@ -322,17 +351,21 @@
             pltpu.VMEM((count, width), bf16),
             pltpu.VMEM((count, width), bf16),
         ] + [pltpu.VMEM((share, width), bf16)] * 7 + [
-            dma((7,)), dma((2,)), dma((1,)), dma((5, 3)), dma((5, 3)), dma((2,)), dma((2,)),
+            dma((5,)), dma((2,)), dma((1,)), dma((7, 3)), dma((7, 3)), dma((4,)), dma((4,)),
             dma((patches - 1,)), dma((patches - 1,)), dma((patches - 1,)), dma((patches - 1,)),
-            dma((4,)), dma((4,)), dma((2, 3)), dma((2, 3)),
+            dma((6,)), dma((6,)), dma((4, 3)), dma((4, 3)),
         ],
         compiler_params=pltpu.CompilerParams(
             collective_id=0, has_side_effects=True, vmem_limit_bytes=60 * 1024 * 1024
         ),
     )(
-        nodes, halo_rows.reshape(-1, 1), coarse, edge_count.reshape(1, 1),
-        receivers.reshape(1, -1), vecs,
-        senders.reshape(-1, 1), receivers.reshape(-1, 1), edges,
+        nodes, halo_rows.reshape(2, border), coarse, edge_count.reshape(1, 1),
+        senders.reshape(1, -1), receivers.reshape(1, -1),
+        b_edge_in.reshape(1, -1), b_edge_out.reshape(1, -1),
+        edge_gain.reshape(1, -1), edge_shift.reshape(1, -1),
+        b_node_in.reshape(1, -1), b_node_out.reshape(1, -1),
+        node_gain.reshape(1, -1), node_shift.reshape(1, -1),
+        edges,
         w_edge_in, w_edge_out, w_node_in, w_node_out,
     )
 

time: 86.1 us -> 75.3 us (0.87)
  local copies, waits for them, and re-layouts: 13.3 us -> 6.37 us
  Pallas kernels: 71.2 us -> 67.4 us
    pallas_call x1, Pallas kernels: 71.2 us -> 67.4 us  [local(): pl.pallas_call(functools.partial(kernel, patches, slot, border, block), o...]
    reshape x2 -> x0, local copies, waits for them, and re-layouts: 3.41 us -> none  [the longest x1 2.05 us: local(): senders.reshape(-1, 1)]
    unnamed x6 -> x2, local copies, waits for them, and re-layouts: 6.97 us -> 4.91 us
    another operation x1 -> x0, local copies, waits for them, and re-layouts: 1.42 us -> none  [local(): jnp.stack([b_edge_in, b_edge_out, edge_gain, edge_shift, b_node_in, b_nod...]
where the time goes in v2:
time: 75.3 us; the launch traced here: 75 us
  Pallas kernels  67.4 us (90%)
  local copies, waits for them, and re-layouts  6.37 us (8%)
  between operations  1.29 us (2%)
    pallas_call x1, Pallas kernels, local(): pl.pallas_call(functools.partial(kernel, patches, slot, border, block), o...  67.4 us
    unnamed x2, local copies, waits for them, and re-layouts  4.91 us

profile of v2, /device:TPU:0, one launch (start us, length us, event | category | flops | bytes accessed | tf_op | source)
XLA Modules:
  0.0 75.0 jit_solution(9621308622130150359)
XLA Ops:
  1.3 0.8 %broadcast_in_dim.7 = s32[64]{0:T(128)S(1)} reshape(s32[1,8,8]{2,1,0:T(8,128)} %param.24) | data formatting | bytes 512 | tf_op jit(solution)/shard_map/broadcast_in_dim | solution.py:324
  2.0 0.7 broadcast_in_dim.8.coarse
  2.7 67.4 %shard_map.194 = (bf16[2048,128]{1,0:T(8,128)(2,1)}, bf16[2048,512]{1,0:T(8,128)(2,1)}) custom-call(bf16[2048,128]{1,0:T(8,128)(2,1)} %nodes.1, s32[2,1024]{1,0:T(2,128)} %bitcast.13, s32[64,128]{1,0:T(8,128)} %broadcast_in_dim.8.coarse, s32[1,1]{1,0:T(1,128)} %bitcast.12.live, s32[1,2048]{1,0:T(1,128)} %bitcast.14, s32[1,2048]{1,0:T(1,128)} %bitcast.15, ...), custom_call_target="tpu_custom_call" | custom-call | tf_op jit(solution)/shard_map/pallas_call | solution.py:328
  70.1 1.9 %copy.24 = bf16[2048,128]{1,0:T(8,128)(2,1)} copy(bf16[2048,128]{1,0:T(8,128)(2,1)} %get-tuple-element.4) | data formatting | bytes 1048576
  72.0 3.0 %copy.25 = bf16[2048,512]{1,0:T(8,128)(2,1)} copy(bf16[2048,512]{1,0:T(8,128)(2,1)} %get-tuple-element.5) | data formatting | bytes 4194304
